TPU v7x, 32 devices: a whole 2x2x4 slice. The times are simulated.
32 devices in a mesh: row: 8 (over z, x), col: 4 (over y, core).
Axes of the slice: x: 2, y: 2, z: 4, core: 2. Of those that a mesh axis runs over, the one named last changes fastest.
Arguments:
- panel_block: float32 [20480, 512], P('row', 'col'), may hold values from -12 to 12
- trailing: float32 [20480, 20480], P('row', 'col'), may hold values from -6 to 6
Outputs:
- updated: float32 [20480, 20480], P('row', 'col')
All inputs are finite; a program needn't handle non-finite values.
Results may differ from a plain program's by a relative error of at most 0.0003.
Values sent between devices are 32-bit elements; how exact they have to be, the bound alone decides.
No kernel may reach another device: no remote copies, remote signals or barrier semaphores. Data moves between devices by JAX's collectives and lax.ppermute only.
A program may use at most 192 MiB of HBM per device.

v0:
```python
import jax
import jax.numpy as jnp
from jax import lax
from jax.sharding import PartitionSpec as P

N = 20480


def on_device(panel_block, trailing):
    local_rows = panel_block.shape[0]
    local_width = panel_block.shape[1]
    rows_count = lax.axis_size("row")
    cols_count = lax.axis_size("col")
    copies = rows_count // cols_count
    row_owner = lax.axis_index("row")
    col_owner = lax.axis_index("col")
    mc_rows = lax.all_gather(panel_block, "col", axis=1, tiled=True)
    squares = lax.psum(jnp.sum(mc_rows * mc_rows), "row")
    column_block = lax.all_gather(panel_block, "row", axis=0, tiled=True)
    shaped = column_block.reshape(copies, cols_count, local_rows, local_width)
    moved = lax.all_to_all(shaped, "col", split_axis=1, concat_axis=3, tiled=True)
    stacked = moved.reshape(copies, local_rows, mc_rows.shape[1])
    mr_rows = jnp.transpose(stacked, (1, 0, 2)).reshape(copies * local_rows, stacked.shape[2])
    update = lax.dot_general(
        mc_rows,
        mr_rows,
        (((1,), (1,)), ((), ())),
        precision=lax.Precision.HIGHEST,
        preferred_element_type=jnp.float32,
    )
    row_index = jnp.arange(local_rows, dtype=jnp.int32) * rows_count + row_owner
    col_index = jnp.arange(mr_rows.shape[0], dtype=jnp.int32) * cols_count + col_owner
    lower_part = row_index[:, None] >= col_index[None, :]
    factor = 0.8 * jnp.sqrt(jnp.float32(N)) / jnp.sqrt(squares + 1e-06)
    return trailing - factor * jnp.where(lower_part, update, jnp.zeros_like(update))


def solution(mesh):
    in_specs = (P("row", "col"), P("row", "col"))
    out_specs = P("row", "col")
    return jax.shard_map(
        on_device, mesh=mesh, in_specs=in_specs, out_specs=out_specs, check_vma=False
    )
```

profile of v0, /device:TPU:0, one launch (start us, length us, event | category | flops | bytes accessed | tf_op | source)
XLA Modules:
  0.0 456.7 jit_solution(3020572873124051038)
XLA Ops:
  6.5 0.0 all-gather.5.cloned.1.call-start
  6.5 0.7 all-gather.5.cloned.1.call-update
  7.3 0.0 all-gather.3.cloned.1.call-start
  7.3 0.7 all-gather.3.cloned.1.call-update
  8.0 154.8 %all-gather.5.cloned.1.call-done = f32[20480,128]{1,0:T(8,128)} async-done(((f32[2560,128]{1,0:T(8,128)}), f32[20480,128]{1,0:T(8,128)}) %all-gather.5.cloned.1.call-update) | async-done | bytes 10485776 | tf_op jit(solution)/shard_map/all_gather | solution.py:19
  162.8 9.6 %copy.6 = f32[2,4,2560,128]{3,2,0,1:T(8,128)} copy(f32[2,4,2560,128]{3,2,1,0:T(8,128)} %bitcast.11) | data formatting | bytes 20971520 | tf_op jit(solution)/shard_map/reshape | solution.py:20
  172.4 6.0 %all-to-all-start = ((f32[2,4,2560,128]{3,2,0,1:T(8,128)}), f32[2,4,2560,128]{3,2,0,1:T(8,128)}, u32[]{:S(2)}, u32[]{:S(2)}) async-start(f32[2,4,2560,128]{3,2,0,1:T(8,128)} %copy.6), calls=%async_computation | async-start | bytes 20971520 | tf_op jit(solution)/shard_map/all_to_all | solution.py:21
  178.5 45.0 %all-gather.3.cloned.1.call-done = f32[2560,512]{1,0:T(8,128)} async-done(((f32[2560,128]{1,0:T(8,128)}), f32[2560,512]{1,0:T(8,128)}) %all-gather.3.cloned.1.call-update) | async-done | bytes 5242896 | tf_op jit(solution)/shard_map/all_gather | solution.py:17
  223.4 4.5 multiply_reduce_fusion
  227.9 25.2 %psum.7 = f32[]{:T(128)} all-reduce(f32[]{:T(128)} %multiply_reduce_fusion), channel_id=1, replica_groups=mesh['row'=8,'col'=4] {'row'}, use_global_device_ids=true, to_apply=%region_1.0 | all-reduce | flops 1 | bytes 8 | tf_op jit(solution)/shard_map/psum | solution.py:18
  253.8 60.0 %all-to-all-done = f32[2,4,2560,128]{3,2,0,1:T(8,128)} async-done(((f32[2,4,2560,128]{3,2,0,1:T(8,128)}), f32[2,4,2560,128]{3,2,0,1:T(8,128)}, u32[]{:S(2)}, u32[]{:S(2)}) %all-to-all-start) | async-done | bytes 10485792 | tf_op jit(solution)/shard_map/all_to_all | solution.py:21
  313.8 11.4 %copy.7 = f32[2,4,2560,128]{2,3,1,0:T(8,128)} copy(f32[2,4,2560,128]{3,2,0,1:T(8,128)} %all-to-all-done) | data formatting | bytes 20971520 | tf_op jit(solution)/shard_map/all_to_all | solution.py:21
  325.2 16.1 %copy.8 = f32[2560,2,512]{2,1,0:T(2,128)} copy(f32[2560,2,512]{0,2,1:T(8,128)} %bitcast.10) | data formatting | bytes 20971520 | tf_op jit(solution)/shard_map/transpose | solution.py:23
  341.3 13.3 %reshape.22 = f32[5120,512]{1,0:T(8,128)} reshape(f32[2560,2,512]{2,1,0:T(2,128)} %copy.8) | data formatting | bytes 20971520 | tf_op jit(solution)/shard_map/reshape | solution.py:23
  354.5 95.4 %multiply_subtract_fusion = f32[2560,5120]{1,0:T(8,128)} fusion(f32[2560,5120]{1,0:T(8,128)} %param.3, f32[2560,512]{1,0:T(8,128)} %all-gather.3.cloned.1.call-done, f32[5120,512]{1,0:T(8,128)} %reshape.22, s32[5120]{0:T(1024)S(1)} %multiply_add_fusion, f32[]{:T(128)S(6)} %div.3, s32[2560]{0:T(1024)S(1)} %multiply_add_fusion.1), kind=kOutput, calls=%fused_computation | convolution fusion | flops 80583065600 | bytes 120616960 | tf_op jit(solution)/shard_map/dot_general | solution.py:24
  (2 shorter events, 0.0 us)
Async XLA Ops:
  6.5 156.2 %all-gather.5.cloned.1.call-start = ((), (), s32[]{:S(2)}) async-start(), calls=%async_computation.2 | async-start | bytes 11796480 | tf_op jit(solution)/shard_map/all_gather | solution.py:19
  7.3 216.2 %all-gather.3.cloned.1.call-start = ((), (), s32[]{:S(2)}) async-start(), calls=%async_computation.1 | async-start | bytes 6553600 | tf_op jit(solution)/shard_map/all_gather | solution.py:17
  172.4 141.4 %all-to-all-start = ((f32[2,4,2560,128]{3,2,0,1:T(8,128)}), f32[2,4,2560,128]{3,2,0,1:T(8,128)}, u32[]{:S(2)}, u32[]{:S(2)}) async-start(f32[2,4,2560,128]{3,2,0,1:T(8,128)} %copy.6), calls=%async_computation | async-start | bytes 20971520 | tf_op jit(solution)/shard_map/all_to_all | solution.py:21
Sparse Core Ops, SparseCore 0:
  9.5 153.2 all-gather.4
  164.3 59.0 all-gather.2
where the time goes:
time: 458 us; the launch traced here: 457 us
  waiting for transfers between devices  261 us (57%)
  matrix products  95.4 us (21%)
  local copies, waits for them, and re-layouts  50.4 us (11%)
  blocking collectives  25.2 us (6%)
  between operations  14.1 us (3%)
  starting transfers between devices  6.08 us (1%)
    all_gather x1, waiting for transfers between devices, on_device(): column_block = lax.all_gather(panel_block, 'row', axis=0, tiled=True)  155 us
    dot_general x1, matrix products, on_device(): lax.dot_general(mc_rows, mr_rows, (((1,), (1,)), ((), ())), precision=lax...  95.4 us
    all_to_all x1, waiting for transfers between devices, on_device(): lax.all_to_all(shaped, 'col', split_axis=1, concat_axis=3, tiled=True)  60 us
    all_gather x1, waiting for transfers between devices, on_device(): mc_rows = lax.all_gather(panel_block, 'col', axis=1, tiled=True)  45 us
    psum x1, blocking collectives, on_device(): squares = lax.psum(jnp.sum(mc_rows * mc_rows), 'row')  25.2 us
    transpose x1, local copies, waits for them, and re-layouts, on_device(): jnp.transpose(stacked, (1, 0, 2))  16.1 us
    reshape x1, local copies, waits for them, and re-layouts, on_device(): jnp.transpose(stacked, (1, 0, 2))  13.3 us
    all_to_all x1, local copies, waits for them, and re-layouts, on_device(): lax.all_to_all(shaped, 'col', split_axis=1, concat_axis=3, tiled=True)  11.4 us
  transfers between devices with their start and end apart: 3, of which 3 were waited for; matrix products, arithmetic and copies ran while one was open for 3% of the time, Pallas kernels for 0%

commit v1 on v0

--- a/solution.py
+++ b/solution.py
@@ -16,7 +16,12 @@
     col_owner = lax.axis_index("col")
     mc_rows = lax.all_gather(panel_block, "col", axis=1, tiled=True)
     squares = lax.psum(jnp.sum(mc_rows * mc_rows), "row")
-    column_block = lax.all_gather(panel_block, "row", axis=0, tiled=True)
+    ring = [panel_block]
+    for hop in range(7):
+        ring.append(lax.ppermute(ring[-1], "row", [(dev, (dev + 1) % 8) for dev in range(8)]))
+    column_block = jnp.roll(
+        jnp.concatenate(ring[::-1], axis=0), (lax.axis_index("row") + 1) * ring[0].shape[0], axis=0
+    )
     shaped = column_block.reshape(copies, cols_count, local_rows, local_width)
     moved = lax.all_to_all(shaped, "col", split_axis=1, concat_axis=3, tiled=True)
     stacked = moved.reshape(copies, local_rows, mc_rows.shape[1])

time: 458 us -> 568 us (1.24)
  local copies, waits for them, and re-layouts: 50.4 us -> 168 us
  blocking collectives: 25.2 us -> 17.8 us
    ppermute x0 -> x7, waiting for transfers between devices: none -> 215 us  [on_device(): lax.ppermute(ring[-1], 'row', [(dev, (dev + 1) % 8) for dev in range(8)])]
    all_gather x1 -> x0, waiting for transfers between devices: 155 us -> none  [on_device(): column_block = lax.all_gather(panel_block, 'row', axis=0, tiled=True)]
    unnamed x0 -> x34, local copies, waits for them, and re-layouts: none -> 69.5 us
    sub x0 -> x1, local copies, waits for them, and re-layouts: none -> 52 us  [on_device(): trailing - factor * jnp.where(lower_part, update, jnp.zeros_like(update))]
    all_gather x1, waiting for transfers between devices: 45 us -> 0.02 us  [on_device(): mc_rows = lax.all_gather(panel_block, 'col', axis=1, tiled=True)]
    all_to_all x1, waiting for transfers between devices: 60 us -> 40.5 us  [on_device(): lax.all_to_all(shaped, 'col', split_axis=1, concat_axis=3, tiled=True)]
    psum x1, blocking collectives: 25.2 us -> 17.8 us  [on_device(): squares = lax.psum(jnp.sum(mc_rows * mc_rows), 'row')]
  transfers between devices with their start and end apart: 3 -> 9, of which waited for: 3 -> 8; matrix products, arithmetic and copies ran while one was open for 3% -> 13% of each run, Pallas kernels for 0% -> 0%
where the time goes in v1:
time: 568 us; the launch traced here: 565 us
  waiting for transfers between devices  256 us (45%)
  local copies, waits for them, and re-layouts  168 us (30%)
  matrix products  95.4 us (17%)
  blocking collectives  17.8 us (3%)
  between operations  14.4 us (3%)
  starting transfers between devices  8.97 us (2%)
    ppermute x7, waiting for transfers between devices, on_device(): lax.ppermute(ring[-1], 'row', [(dev, (dev + 1) % 8) for dev in range(8)])  215 us
    dot_general x1, matrix products, on_device(): lax.dot_general(mc_rows, mr_rows, (((1,), (1,)), ((), ())), precision=lax...  95.4 us
    unnamed x34, local copies, waits for them, and re-layouts  69.5 us
    sub x1, local copies, waits for them, and re-layouts, on_device(): trailing - factor * jnp.where(lower_part, update, jnp.zeros_like(update))  52 us
    all_to_all x1, waiting for transfers between devices, on_device(): lax.all_to_all(shaped, 'col', split_axis=1, concat_axis=3, tiled=True)  40.5 us
    psum x1, blocking collectives, on_device(): squares = lax.psum(jnp.sum(mc_rows * mc_rows), 'row')  17.8 us
    transpose x1, local copies, waits for them, and re-layouts, on_device(): jnp.transpose(stacked, (1, 0, 2))  16.1 us
    reshape x1, local copies, waits for them, and re-layouts, on_device(): jnp.transpose(stacked, (1, 0, 2))  13.2 us
  transfers between devices with their start and end apart: 9, of which 8 were waited for; matrix products, arithmetic and copies ran while one was open for 13% of the time, Pallas kernels for 0%

profile of v1, /device:TPU:0, one launch (start us, length us, event | category | flops | bytes accessed | tf_op | source)
XLA Modules:
  0.0 564.9 jit_solution(18077770429059884299)
XLA Ops:
  6.5 3.0 collective-permute-start
  9.5 32.1 %collective-permute-done = f32[2560,128]{1,0:T(8,128)S(1)} collective-permute-done((f32[2560,128]{1,0:T(8,128)}, f32[2560,128]{1,0:T(8,128)S(1)}, u32[]{:S(2)}, u32[]{:S(2)}) %collective-permute-start) | collective-permute-done | bytes 1310752 | tf_op jit(solution)/shard_map/ppermute | solution.py:21
  41.6 0.0 collective-permute-start.1
  41.6 32.6 %collective-permute-done.1 = f32[2560,128]{1,0:T(8,128)S(1)} collective-permute-done((f32[2560,128]{1,0:T(8,128)S(1)}, f32[2560,128]{1,0:T(8,128)S(1)}, u32[]{:S(2)}, u32[]{:S(2)}) %collective-permute-start.1) | collective-permute-done | bytes 1310752 | tf_op jit(solution)/shard_map/ppermute | solution.py:21
  74.2 1.1 copy-done.1
  75.3 0.0 collective-permute-start.2
  75.3 31.8 %collective-permute-done.2 = f32[2560,128]{1,0:T(8,128)S(1)} collective-permute-done((f32[2560,128]{1,0:T(8,128)S(1)}, f32[2560,128]{1,0:T(8,128)S(1)}, u32[]{:S(2)}, u32[]{:S(2)}) %collective-permute-start.2) | collective-permute-done | bytes 1310752 | tf_op jit(solution)/shard_map/ppermute | solution.py:21
  107.1 1.1 copy-done.3
  108.2 0.0 collective-permute-start.3
  108.2 30.9 %collective-permute-done.3 = f32[2560,128]{1,0:T(8,128)S(1)} collective-permute-done((f32[2560,128]{1,0:T(8,128)S(1)}, f32[2560,128]{1,0:T(8,128)S(1)}, u32[]{:S(2)}, u32[]{:S(2)}) %collective-permute-start.3) | collective-permute-done | bytes 1310752 | tf_op jit(solution)/shard_map/ppermute | solution.py:21
  139.1 1.1 copy-done.5
  140.1 0.0 collective-permute-start.4
  140.1 30.1 %collective-permute-done.4 = f32[2560,128]{1,0:T(8,128)S(1)} collective-permute-done((f32[2560,128]{1,0:T(8,128)S(1)}, f32[2560,128]{1,0:T(8,128)S(1)}, u32[]{:S(2)}, u32[]{:S(2)}) %collective-permute-start.4) | collective-permute-done | bytes 1310752 | tf_op jit(solution)/shard_map/ppermute | solution.py:21
  170.2 1.1 copy-done.7
  171.3 0.0 collective-permute-start.5
  171.3 29.3 %collective-permute-done.5 = f32[2560,128]{1,0:T(8,128)} collective-permute-done((f32[2560,128]{1,0:T(8,128)S(1)}, f32[2560,128]{1,0:T(8,128)}, u32[]{:S(2)}, u32[]{:S(2)}) %collective-permute-start.5) | collective-permute-done | bytes 1310752 | tf_op jit(solution)/shard_map/ppermute | solution.py:21
  200.6 0.0 all-gather.2.cloned.1.call-update
  200.7 0.0 copy-start.8
  200.7 28.6 %collective-permute-done.6 = f32[2560,128]{1,0:T(8,128)} collective-permute-done((f32[2560,128]{1,0:T(8,128)}, f32[2560,128]{1,0:T(8,128)}, u32[]{:S(2)}, u32[]{:S(2)}) %collective-permute-start.6) | collective-permute-done | bytes 1310752 | tf_op jit(solution)/shard_map/ppermute | solution.py:21
  229.3 1.4 constant_dynamic-update-slice_fusion.15
  230.7 1.4 constant_dynamic-update-slice_fusion.14
  232.1 1.4 constant_dynamic-update-slice_fusion.13
  233.5 1.4 constant_dynamic-update-slice_fusion.12
  234.9 1.4 constant_dynamic-update-slice_fusion.11
  236.3 1.4 constant_dynamic-update-slice_fusion.10
  237.7 0.1 constant_dynamic-update-slice_fusion.9
  237.8 1.4 constant_dynamic-update-slice_fusion.8
  239.2 1.4 constant_dynamic-update-slice_fusion.7
  240.6 1.5 constant_dynamic-update-slice_fusion.6
  242.1 0.1 constant_dynamic-update-slice_fusion.5
  242.2 0.1 constant_dynamic-update-slice_fusion.4
  242.3 0.1 constant_dynamic-update-slice_fusion.3
  242.4 0.1 constant_dynamic-update-slice_fusion.2
  242.5 0.1 constant_dynamic-update-slice_fusion.1
  242.6 0.1 constant_dynamic-update-slice_fusion
  242.7 0.9 constant_dynamic-slice_fusion
  243.6 4.5 copy.12
  248.2 6.0 %all-to-all-start = ((f32[2,4,2560,128]{3,2,0,1:T(8,128)}), f32[2,4,2560,128]{3,2,0,1:T(8,128)}, u32[]{:S(2)}, u32[]{:S(2)}) async-start(f32[2,4,2560,128]{3,2,0,1:T(8,128)} %copy.12), calls=%async_computation | async-start | bytes 20971520 | tf_op jit(solution)/shard_map/all_to_all | solution.py:26
  254.2 0.0 all-gather.2.cloned.1.call-done
  254.2 4.5 multiply_reduce_fusion
  258.7 52.0 %copy.15 = f32[2560,5120]{0,1:T(8,128)} copy(f32[2560,5120]{1,0:T(8,128)} %param.3) | data formatting | bytes 104857600 | tf_op args[1]
  310.8 17.8 %psum.7 = f32[]{:T(128)} all-reduce(f32[]{:T(128)} %multiply_reduce_fusion), channel_id=1, replica_groups=mesh['row'=8,'col'=4] {'row'}, use_global_device_ids=true, to_apply=%region_1.0 | all-reduce | flops 1 | bytes 8 | tf_op jit(solution)/shard_map/psum | solution.py:18
  329.3 40.5 %all-to-all-done = f32[2,4,2560,128]{3,2,0,1:T(8,128)} async-done(((f32[2,4,2560,128]{3,2,0,1:T(8,128)}), f32[2,4,2560,128]{3,2,0,1:T(8,128)}, u32[]{:S(2)}, u32[]{:S(2)}) %all-to-all-start) | async-done | bytes 10485792 | tf_op jit(solution)/shard_map/all_to_all | solution.py:26
  369.8 11.5 %copy.13 = f32[2,4,2560,128]{2,3,1,0:T(8,128)} copy(f32[2,4,2560,128]{3,2,0,1:T(8,128)} %all-to-all-done) | data formatting | bytes 20971520 | tf_op jit(solution)/shard_map/all_to_all | solution.py:26
  381.2 16.1 %copy.14 = f32[2560,2,512]{2,1,0:T(2,128)} copy(f32[2560,2,512]{0,2,1:T(8,128)} %bitcast.17) | data formatting | bytes 20971520 | tf_op jit(solution)/shard_map/transpose | solution.py:28
  397.4 13.2 %reshape.22 = f32[5120,512]{1,0:T(8,128)} reshape(f32[2560,2,512]{2,1,0:T(2,128)} %copy.14) | data formatting | bytes 20971520 | tf_op jit(solution)/shard_map/reshape | solution.py:28
  410.6 95.4 %fusion.1 = f32[2560,5120]{0,1:T(8,128)} fusion(f32[2560,5120]{0,1:T(8,128)} %copy.15, f32[5120,512]{1,0:T(8,128)} %reshape.22, f32[2560,512]{1,0:T(8,128)} %all-gather.2.cloned.1.call-done, s32[2560]{0:T(1024)S(1)} %multiply_add_fusion.1, f32[]{:T(128)S(6)} %div.3, s32[5120]{0:T(1024)S(1)} %multiply_add_fusion), kind=kOutput, calls=%fused_computation.2 | convolution fusion | flops 80583065600 | bytes 120616960 | tf_op jit(solution)/shard_map/dot_general | solution.py:29
  506.0 52.0 %copy.16 = f32[2560,5120]{1,0:T(8,128)} copy(f32[2560,5120]{0,1:T(8,128)} %fusion.1) | data formatting | bytes 104857600 | tf_op jit(solution)/shard_map/sub | solution.py:40
  (17 shorter events, 0.0 us)
Async XLA Ops:
  6.5 236.1 %copy-start = (f32[2560,128]{1,0:T(8,128)S(1)}, f32[2560,128]{1,0:T(8,128)}, u32[]{:S(2)}) copy-start(f32[2560,128]{1,0:T(8,128)} %param.2) | copy-start | bytes 3932164
  6.5 247.7 %all-gather.2.cloned.1.call-start = ((), (), s32[]{:S(2)}) async-start(), calls=%async_computation.1 | async-start | bytes 6553600 | tf_op jit(solution)/shard_map/all_gather | solution.py:17
  6.5 35.1 %collective-permute-start = (f32[2560,128]{1,0:T(8,128)}, f32[2560,128]{1,0:T(8,128)S(1)}, u32[]{:S(2)}, u32[]{:S(2)}) collective-permute-start(f32[2560,128]{1,0:T(8,128)} %param.2), channel_id=1, source_target_pairs={{0,4},{4,8},{8,12},{12,16},{16,20},{20,24},{24,28},{28,0},{1,5},{5... | collective-permute-start | bytes 3932168 | tf_op jit(solution)/shard_map/ppermute | solution.py:21
  41.6 32.6 %collective-permute-start.1 = (f32[2560,128]{1,0:T(8,128)S(1)}, f32[2560,128]{1,0:T(8,128)S(1)}, u32[]{:S(2)}, u32[]{:S(2)}) collective-permute-start(f32[2560,128]{1,0:T(8,128)S(1)} %collective-permute-done), channel_id=1, source_target_pairs={{0,4},{4,8},{8,12},{12,16},{16,20},{20,24},{24,28},{28,0},{1,5},{5... | collective-permute-start | bytes 3932168 | tf_op jit(solution)/shard_map/ppermute | solution.py:21
  74.2 1.1 copy-start.1
  75.3 31.8 %collective-permute-start.2 = (f32[2560,128]{1,0:T(8,128)S(1)}, f32[2560,128]{1,0:T(8,128)S(1)}, u32[]{:S(2)}, u32[]{:S(2)}) collective-permute-start(f32[2560,128]{1,0:T(8,128)S(1)} %collective-permute-done.1), channel_id=1, source_target_pairs={{0,4},{4,8},{8,12},{12,16},{16,20},{20,24},{24,28},{28,0},{1,5},{5... | collective-permute-start | bytes 3932168 | tf_op jit(solution)/shard_map/ppermute | solution.py:21
  107.1 1.1 copy-start.3
  108.2 30.9 %collective-permute-start.3 = (f32[2560,128]{1,0:T(8,128)S(1)}, f32[2560,128]{1,0:T(8,128)S(1)}, u32[]{:S(2)}, u32[]{:S(2)}) collective-permute-start(f32[2560,128]{1,0:T(8,128)S(1)} %collective-permute-done.2), channel_id=1, source_target_pairs={{0,4},{4,8},{8,12},{12,16},{16,20},{20,24},{24,28},{28,0},{1,5},{5... | collective-permute-start | bytes 3932168 | tf_op jit(solution)/shard_map/ppermute | solution.py:21
  139.1 1.1 copy-start.5
  140.1 30.1 %collective-permute-start.4 = (f32[2560,128]{1,0:T(8,128)S(1)}, f32[2560,128]{1,0:T(8,128)S(1)}, u32[]{:S(2)}, u32[]{:S(2)}) collective-permute-start(f32[2560,128]{1,0:T(8,128)S(1)} %collective-permute-done.3), channel_id=1, source_target_pairs={{0,4},{4,8},{8,12},{12,16},{16,20},{20,24},{24,28},{28,0},{1,5},{5... | collective-permute-start | bytes 3932168 | tf_op jit(solution)/shard_map/ppermute | solution.py:21
  170.2 1.1 copy-start.7
  171.3 29.3 %collective-permute-start.5 = (f32[2560,128]{1,0:T(8,128)S(1)}, f32[2560,128]{1,0:T(8,128)}, u32[]{:S(2)}, u32[]{:S(2)}) collective-permute-start(f32[2560,128]{1,0:T(8,128)S(1)} %collective-permute-done.4), channel_id=1, source_target_pairs={{0,4},{4,8},{8,12},{12,16},{16,20},{20,24},{24,28},{28,0},{1,5},{5... | collective-permute-start | bytes 3932168 | tf_op jit(solution)/shard_map/ppermute | solution.py:21
  200.6 28.7 %collective-permute-start.6 = (f32[2560,128]{1,0:T(8,128)}, f32[2560,128]{1,0:T(8,128)}, u32[]{:S(2)}, u32[]{:S(2)}) collective-permute-start(f32[2560,128]{1,0:T(8,128)} %collective-permute-done.5), channel_id=1, source_target_pairs={{0,4},{4,8},{8,12},{12,16},{16,20},{20,24},{24,28},{28,0},{1,5},{5... | collective-permute-start | bytes 3932168 | tf_op jit(solution)/shard_map/ppermute | solution.py:21
  200.7 41.5 %copy-start.8 = (f32[2560,128]{1,0:T(8,128)S(1)}, f32[2560,128]{1,0:T(8,128)}, u32[]{:S(2)}) copy-start(f32[2560,128]{1,0:T(8,128)} %copy-done.7) | copy-start | bytes 3932164
  200.7 41.6 %copy-start.6 = (f32[2560,128]{1,0:T(8,128)S(1)}, f32[2560,128]{1,0:T(8,128)}, u32[]{:S(2)}) copy-start(f32[2560,128]{1,0:T(8,128)} %copy-done.5) | copy-start | bytes 3932164
  200.7 41.7 %copy-start.4 = (f32[2560,128]{1,0:T(8,128)S(1)}, f32[2560,128]{1,0:T(8,128)}, u32[]{:S(2)}) copy-start(f32[2560,128]{1,0:T(8,128)} %copy-done.3) | copy-start | bytes 3932164
  200.7 41.7 %copy-start.2 = (f32[2560,128]{1,0:T(8,128)S(1)}, f32[2560,128]{1,0:T(8,128)}, u32[]{:S(2)}) copy-start(f32[2560,128]{1,0:T(8,128)} %copy-done.1) | copy-start | bytes 3932164
  248.2 121.6 %all-to-all-start = ((f32[2,4,2560,128]{3,2,0,1:T(8,128)}), f32[2,4,2560,128]{3,2,0,1:T(8,128)}, u32[]{:S(2)}, u32[]{:S(2)}) async-start(f32[2,4,2560,128]{3,2,0,1:T(8,128)} %copy.12), calls=%async_computation | async-start | bytes 20971520 | tf_op jit(solution)/shard_map/all_to_all | solution.py:26
Sparse Core Ops, SparseCore 0:
  200.7 41.8 all-gather.1
